TPU v7x, 32 devices: a whole 2x2x4 slice. The times are simulated.
32 devices in a mesh: section: 2 (over core), vocab: 16 (over z, y, x).
Axes of the slice: x: 2, y: 2, z: 4, core: 2. Of those that a mesh axis runs over, the one named last changes fastest.
Arguments:
- hidden_in: bfloat16 [2, 256, 7168], P(None, ('section', 'vocab')), may hold values from -6 to 6
- gain_ffn: float32 [7168], replicated, may hold values from 0.4 to 1.6
- w_gate: bfloat16 [7168, 18432], P(None, ('section', 'vocab')), may hold values from -0.0625 to 0.0625
- w_up: bfloat16 [7168, 18432], P(None, ('section', 'vocab')), may hold values from -0.0625 to 0.0625
- w_down: bfloat16 [18432, 7168], P(('section', 'vocab')), may hold values from -0.046875 to 0.046875
- gain_final: float32 [7168], replicated, may hold values from 0.4 to 1.6
- head_weight: bfloat16 [7168, 129280], P(None, ('section', 'vocab')), may hold values from -4.5 to 4.5
- sampled_ids: int32 [2, 256], replicated, may hold values from 0 to 129279
- seq_ids: int32 [2, 256], P(None, ('section', 'vocab')), may hold values from 0 to 7, never falling along the last dimension, each value on 1 to 128 neighbouring positions
Outputs:
- token_logprob: float32 [2, 256], P(None, ('section', 'vocab'))
- log_norm: float32 [2, 256], P(None, ('section', 'vocab'))
- top_mass: float32 [2, 256], P(None, ('section', 'vocab'))
- seq_logprob: float32 [2, 8], replicated
All inputs are finite; a program needn't handle non-finite values.
Results may differ from a plain program's by a relative error of at most 0.006.
Values may be sent and summed in bfloat16 or wider, within the bound.
No kernel may reach another device: no remote copies, remote signals or barrier semaphores. Data moves between devices by JAX's collectives and lax.ppermute only.
A program may use at most 192 MiB of HBM per device.

v0:
```python
import jax
import jax.numpy as jnp
from jax import lax
from jax.sharding import PartitionSpec as P

SEQS = 8
TOPK = 20
epsilon = 1e-06


def rms_norm(values, scale_gain):
    wide = values.astype(jnp.float32)
    square_mean = jnp.mean(wide * wide, axis=-1, keepdims=True)
    return (wide * lax.rsqrt(square_mean + epsilon) * scale_gain).astype(jnp.bfloat16)


def largest(values):
    return lax.sort(values, dimension=values.ndim - 1)[..., -TOPK:]


def finish(peak_value, sum_total, sampled_logit, leaders_all):
    log_norm = peak_value + jnp.log(sum_total)
    top_mass = jnp.sum(jnp.exp(leaders_all - log_norm[:, None]), axis=1)
    return (sampled_logit - log_norm, log_norm, top_mass)


def combine_sources(pieces):
    maxima, exp_sums, sampled_parts, top_values = pieces
    peak_value = jnp.max(maxima, axis=0)
    sum_total = jnp.sum(exp_sums * jnp.exp(maxima - peak_value[None, :]), axis=0)
    sampled_logit = jnp.sum(sampled_parts, axis=0)
    item_count = top_values.shape[1]
    pooled = jnp.transpose(top_values, (1, 0, 2)).reshape(item_count, -1)
    leaders_all = largest(pooled)
    return finish(peak_value, sum_total, sampled_logit, leaders_all)


def body(hidden_in, gain_ffn, w_gate, w_up, w_down, gain_final, head_weight, sampled_ids, seq_ids):
    row_count = hidden_in.shape[1]
    shard_width = head_weight.shape[1]
    position = lax.axis_index(("section", "vocab"))
    group_count = lax.axis_size(("section", "vocab"))
    columns = lax.broadcasted_iota(jnp.int32, (1, shard_width), 1) + position * shard_width
    logprob_list = []
    norm_list = []
    mass_list = []
    partials = []
    for microbatch in range(hidden_in.shape[0]):
        own_rows = hidden_in[microbatch]
        gathered = lax.all_gather(own_rows, ("section", "vocab"), axis=0, tiled=True)
        normed = rms_norm(gathered, gain_ffn)
        gate_proj = jnp.dot(normed, w_gate, preferred_element_type=jnp.float32)
        up_proj = jnp.dot(normed, w_up, preferred_element_type=jnp.float32)
        hidden_act = (jax.nn.silu(gate_proj) * up_proj).astype(jnp.bfloat16)
        branch = lax.psum(
            jnp.dot(hidden_act, w_down, preferred_element_type=jnp.float32), ("section", "vocab")
        )
        residual = (gathered.astype(jnp.float32) + branch).astype(jnp.bfloat16)
        scaled = rms_norm(residual, gain_final)
        logits = jnp.dot(scaled, head_weight, preferred_element_type=jnp.float32)
        token_ids = sampled_ids[microbatch]
        matches = columns == token_ids[:, None]
        sampled_part = jnp.sum(jnp.where(matches, logits, 0.0), axis=1)
        leaders = largest(logits)
        local_peak = jnp.max(logits, axis=1).reshape(group_count, row_count)
        local_total = jnp.sum(jnp.exp(logits - jnp.max(logits, axis=1)[:, None]), axis=1).reshape(
            group_count, row_count
        )
        sampled_block = sampled_part.reshape(group_count, row_count)
        leader_block = leaders.reshape(group_count, row_count, TOPK)
        token_logprob, log_norm, top_mass = combine_sources(
            (
                lax.all_to_all(
                    local_peak, ("section", "vocab"), split_axis=0, concat_axis=0, tiled=True
                ),
                lax.all_to_all(
                    local_total, ("section", "vocab"), split_axis=0, concat_axis=0, tiled=True
                ),
                lax.all_to_all(
                    sampled_block, ("section", "vocab"), split_axis=0, concat_axis=0, tiled=True
                ),
                lax.all_to_all(
                    leader_block, ("section", "vocab"), split_axis=0, concat_axis=0, tiled=True
                ),
            )
        )
        onehot = (
            seq_ids[microbatch][:, None] == jnp.arange(SEQS, dtype=jnp.int32)[None, :]
        ).astype(jnp.float32)
        partials.append(jnp.sum(token_logprob[:, None] * onehot, axis=0))
        logprob_list.append(token_logprob)
        norm_list.append(log_norm)
        mass_list.append(top_mass)
    seq_logprob = lax.psum(jnp.stack(partials), ("section", "vocab"))
    return (jnp.stack(logprob_list), jnp.stack(norm_list), jnp.stack(mass_list), seq_logprob)


def solution(mesh):
    in_specs = (
        P(None, ("section", "vocab"), None),
        P(),
        P(None, ("section", "vocab")),
        P(None, ("section", "vocab")),
        P(("section", "vocab"), None),
        P(),
        P(None, ("section", "vocab")),
        P(),
        P(None, ("section", "vocab")),
    )
    out_specs = (
        P(None, ("section", "vocab")),
        P(None, ("section", "vocab")),
        P(None, ("section", "vocab")),
        P(),
    )
    return jax.shard_map(body, mesh=mesh, in_specs=in_specs, out_specs=out_specs, check_vma=False)
```

profile of v0, /device:TPU:0, one launch (start us, length us, event | category | flops | bytes accessed | tf_op | source)
XLA Modules:
  0.0 1247.0 jit_solution(10427038897527076204)
XLA Ops:
  9.7 64.3 %all-gather.5.cloned.1.call-done = bf16[1,256,7168]{2,1,0:T(8,128)(2,1)} async-done(((bf16[1,8,7168]{2,1,0:T(8,128)(2,1)}), bf16[1,256,7168]{2,1,0:T(8,128)(2,1)}) %all-gather.5.cloned.1.call-update) | async-done | bytes 3670032 | tf_op jit(solution)/shard_map/all_gather | solution.py:50
  74.0 2.8 fusion.6
  76.9 59.1 %all-gather.7.cloned.1.call-done = bf16[1,256,7168]{2,1,0:T(8,128)(2,1)} async-done(((bf16[1,8,7168]{2,1,0:T(8,128)(2,1)}), bf16[1,256,7168]{2,1,0:T(8,128)(2,1)}) %all-gather.7.cloned.1.call-update) | async-done | bytes 3670032 | tf_op jit(solution)/shard_map/all_gather | solution.py:50
  135.9 3.0 fusion.10
  139.0 7.0 fusion.28
  146.0 2.4 fusion.25
  148.5 19.7 %fusion.34 = f32[256,7168]{1,0:T(8,128)} fusion(bf16[576,7168]{1,0:T(8,128)(2,1)} %param.13, bf16[7168,576]{0,1:T(8,128)(2,1)} %param.12, bf16[1,256,7168]{2,1,0:T(8,128)(2,1)} %all-gather.5.cloned.1.call-done, f32[7168]{0:T(1024)S(1)} %copy-done.3, f32[256]{0:T(256)S(1)} %add_rsqrt_fusion.3, f32[256,576]{0,1:T(8,128)S(1)} %fusion.28), kind=kOutput, calls=%fused_computation.41 | convolution fusion | flops 4236083200 | bytes 28144640 | tf_op jit(solution)/shard_map/dot_general | solution.py:56
  168.2 19.3 %fusion.31 = f32[256,7168]{1,0:T(8,128)} fusion(bf16[576,7168]{1,0:T(8,128)(2,1)} %param.13, bf16[7168,576]{0,1:T(8,128)(2,1)} %param.12, bf16[1,256,7168]{2,1,0:T(8,128)(2,1)} %all-gather.7.cloned.1.call-done, f32[256]{0:T(256)S(1)} %add_rsqrt_fusion.1, f32[7168]{0:T(1024)S(1)} %copy-done.3, f32[256,576]{0,1:T(8,128)S(1)} %fusion.25), kind=kOutput, calls=%fused_computation.40 | convolution fusion | flops 4236083200 | bytes 28144640 | tf_op jit(solution)/shard_map/dot_general | solution.py:56
  188.2 251.1 %all-reduce.3.cloned.1.call-done = (f32[256,7168]{1,0:T(8,128)}, f32[256,7168]{1,0:T(8,128)}) async-done(((f32[256,7168]{1,0:T(8,128)}, f32[256,7168]{1,0:T(8,128)}), (f32[256,7168]{1,0:T(8,128)}, f32[256,7168]{1,0:T(8,128)})) %all-reduce.3.cloned.1.call-update) | async-done | bytes 14680080 | tf_op jit(solution)/shard_map/psum | solution.py:55
  439.3 8.4 fusion
  447.7 28.2 %fusion.46 = (f32[256]{0:T(256)S(1)}, f32[256,4040]{0,1:T(8,128)}) fusion(bf16[7168,4040]{0,1:T(8,128)(2,1)} %param.15, f32[7168]{0:T(1024)S(1)} %copy-done.4, f32[256]{0:T(256)S(1)} %add_rsqrt_fusion.2, f32[256,7168]{1,0:T(8,128)} %get-tuple-element.25, bf16[1,256,7168]{2,1,0:T(8,128)(2,1)} %all-gather.5.cloned.1.call-done), kind=kOutput, calls=%fused_computation.75 | convolution fusion | flops 14840743936 | bytes 73095168 | tf_op jit(solution)/shard_map/dot_general | solution.py:60
  476.6 4.8 all-to-all-start.1
  483.6 296.8 %sort.56 = (f32[256,4040]{0,1:T(8,128)}, s32[256,4040]{0,1:T(8,128)}) sort(f32[256,4040]{0,1:T(8,128)} %get-tuple-element.39, s32[256,4040]{0,1:T(8,128)} %iota.24.clone), dimensions={1}, to_apply=%region_18.19 | sort | flops 20684800 | bytes 16547840 | tf_op jit(solution)/shard_map/sort | solution.py:18
  780.4 5.6 copy.39
  786.0 28.4 %fusion.47 = (f32[256]{0:T(256)S(1)}, f32[256,4040]{0,1:T(8,128)}) fusion(bf16[7168,4040]{0,1:T(8,128)(2,1)} %param.15, f32[256]{0:T(256)S(1)} %add_rsqrt_fusion, f32[7168]{0:T(1024)S(1)} %copy-done.4, f32[256,7168]{1,0:T(8,128)} %get-tuple-element.24, bf16[1,256,7168]{2,1,0:T(8,128)(2,1)} %all-gather.7.cloned.1.call-done), kind=kOutput, calls=%fused_computation.76 | convolution fusion | flops 14840743936 | bytes 73095168 | tf_op jit(solution)/shard_map/dot_general | solution.py:60
  814.3 5.1 exponential_reduce_fusion.1
  820.4 296.9 %sort.58 = (f32[256,4040]{0,1:T(8,128)}, s32[256,4040]{0,1:T(8,128)}) sort(f32[256,4040]{0,1:T(8,128)} %get-tuple-element.41, s32[256,4040]{0,1:T(8,128)} %iota.24.clone), dimensions={1}, to_apply=%region_21.22 | sort | flops 20684800 | bytes 16547840 | tf_op jit(solution)/shard_map/sort | solution.py:18
  1117.9 5.5 copy.43
  1123.5 5.9 all-to-all-start.2
  1136.6 4.0 all-to-all-start
  1140.6 7.1 all-to-all-done
  1147.8 2.5 all-to-all-start.4
  1150.3 7.1 all-to-all-done.4
  1157.4 2.5 all-to-all-start.5
  1160.0 7.1 all-to-all-done.5
  1167.1 2.5 all-to-all-start.3
  1169.6 7.1 all-to-all-done.3
  1176.7 2.5 all-to-all-start.6
  1180.6 40.4 %psum.23 = f32[2,8]{1,0:T(2,128)} all-reduce(f32[2,8]{1,0:T(2,128)S(1)} %pad_maximum_fusion.3), channel_id=1, replica_groups=mesh['section'=2,'vocab'=16] {'section','vocab'}, use_global_device_ids=true, to_apply=%region_26.27 | all-reduce | flops 16 | bytes 128 | tf_op jit(solution)/shard_map/psum | solution.py:94
  1221.0 5.0 all-to-all-start.7
  1227.6 4.9 sort.57
  1234.3 4.9 sort.59
  (73 shorter events, 20.5 us)
Async XLA Ops:
  7.2 131.8 %copy-start.3 = (f32[7168]{0:T(1024)S(1)}, f32[7168]{0:T(1024)}, u32[]{:S(2)}) copy-start(f32[7168]{0:T(1024)} %param.10) | copy-start | bytes 86020
  7.2 66.8 %all-gather.5.cloned.1.call-start = ((), (), s32[]{:S(2)}) async-start(), calls=%async_computation.8 | async-start | bytes 3784704 | tf_op jit(solution)/shard_map/all_gather | solution.py:50
  8.9 127.0 %all-gather.7.cloned.1.call-start = ((), (), s32[]{:S(2)}) async-start(), calls=%async_computation.9 | async-start | bytes 3784704 | tf_op jit(solution)/shard_map/all_gather | solution.py:50
  9.6 429.6 %all-reduce.3.cloned.1.call-start = ((), (), s32[]{:S(2)}) async-start(), calls=%async_computation.10 | async-start | bytes 29360128 | tf_op jit(solution)/shard_map/psum | solution.py:55
  135.9 10.1 slice-start
  138.9 7.1 copy-start
  139.0 7.1 slice-start.1
  187.5 0.7 copy-start.2
  187.5 0.7 copy-start.1
  439.3 8.4 copy-start.4
  476.6 646.9 %all-to-all-start.1 = ((f32[32,1,8]{2,1,0:T(1,128)}), f32[32,1,8]{2,1,0:T(1,128)S(1)}, u32[]{:S(2)}, u32[]{:S(2)}) async-start(f32[32,1,8]{2,1,0:T(1,128)} %bitcast.5), calls=%async_computation.1 | async-start | bytes 32768 | tf_op jit(solution)/shard_map/all_to_all | solution.py:73
  1123.5 13.1 %all-to-all-start.2 = ((f32[32,1,8]{2,1,0:T(1,128)}), f32[32,1,8]{2,1,0:T(1,128)S(1)}, u32[]{:S(2)}, u32[]{:S(2)}) async-start(f32[32,1,8]{2,1,0:T(1,128)} %bitcast.6), calls=%async_computation.2 | async-start | bytes 32768 | tf_op jit(solution)/shard_map/all_to_all | solution.py:76
  1136.6 11.2 all-to-all-start
  1147.8 9.7 all-to-all-start.4
  1157.4 9.6 all-to-all-start.5
  1167.1 9.6 all-to-all-start.3
  1176.7 44.3 %all-to-all-start.6 = ((f32[32,1,160]{2,1,0:T(1,128)}), f32[32,1,160]{2,1,0:T(1,128)S(1)}, u32[]{:S(2)}, u32[]{:S(2)}) async-start(f32[32,1,160]{2,1,0:T(1,128)} %reshape.189), calls=%async_computation.6 | async-start | bytes 65536 | tf_op jit(solution)/shard_map/all_to_all | solution.py:82
  1221.0 12.2 all-to-all-start.7
Sparse Core Ops, SparseCore 0:
  10.8 63.1 all-gather.4
  76.9 59.0 all-gather.6
  187.7 251.5 all-reduce.2
where the time goes:
time: 1260 us; the launch traced here: 1250 us
  other arithmetic  627 us (50%)
  waiting for transfers between devices  406 us (32%)
  matrix products  105 us (8%)
  blocking collectives  40.4 us (3%)
  starting transfers between devices  29.9 us (2%)
  local copies, waits for them, and re-layouts  24.3 us (2%)
  between operations  14.5 us (1%)
    sort x4, other arithmetic, largest(): return lax.sort(values, dimension=values.ndim - 1)[..., -TOPK:]  604 us
    psum x1, waiting for transfers between devices, body(): lax.psum(jnp.dot(hidden_act, w_down, preferred_element_type=jnp.float32),...  251 us
    all_gather x2, waiting for transfers between devices, body(): lax.all_gather(own_rows, ('section', 'vocab'), axis=0, tiled=True)  123 us
    dot_general x2, matrix products, body(): logits = jnp.dot(scaled, head_weight, preferred_element_type=jnp.float32)  56.6 us
    psum x1, blocking collectives, body(): seq_logprob = lax.psum(jnp.stack(partials), ('section', 'vocab'))  40.4 us
    dot_general x2, matrix products, body(): jnp.dot(hidden_act, w_down, preferred_element_type=jnp.float32)  39 us
  transfers between devices with their start and end apart: 11, of which 9 were waited for; matrix products, arithmetic and copies ran while one was open for 53% of the time, Pallas kernels for 0%

commit v1 on v0

--- a/solution.py
+++ b/solution.py
@@ -53,7 +53,8 @@
         up_proj = jnp.dot(normed, w_up, preferred_element_type=jnp.float32)
         hidden_act = (jax.nn.silu(gate_proj) * up_proj).astype(jnp.bfloat16)
         branch = lax.psum(
-            jnp.dot(hidden_act, w_down, preferred_element_type=jnp.float32), ("section", "vocab")
+            lax.psum(jnp.dot(hidden_act, w_down, preferred_element_type=jnp.float32), "section"),
+            "vocab",
         )
         residual = (gathered.astype(jnp.float32) + branch).astype(jnp.bfloat16)
         scaled = rms_norm(residual, gain_final)

time: 1260 us -> 1470 us (1.17)
  waiting for transfers between devices: 406 us -> 621 us
    psum x0 -> x1, waiting for transfers between devices: none -> 413 us  [body(): lax.psum(lax.psum(jnp.dot(hidden_act, w_down, preferred_element_type=jnp....]
    psum x1, waiting for transfers between devices: 251 us -> 52.2 us  [body(): lax.psum(jnp.dot(hidden_act, w_down, preferred_element_type=jnp.float32),...]
  transfers between devices with their start and end apart: 11 -> 12, of which waited for: 9 -> 10; matrix products, arithmetic and copies ran while one was open for 53% -> 24% of each run, Pallas kernels for 0% -> 0%
where the time goes in v1:
time: 1470 us; the launch traced here: 1460 us
  other arithmetic  627 us (43%)
  waiting for transfers between devices  621 us (42%)
  matrix products  105 us (7%)
  blocking collectives  40.4 us (3%)
  starting transfers between devices  28.7 us (2%)
  local copies, waits for them, and re-layouts  24.3 us (2%)
    sort x4, other arithmetic, largest(): return lax.sort(values, dimension=values.ndim - 1)[..., -TOPK:]  604 us
    psum x1, waiting for transfers between devices, body(): lax.psum(lax.psum(jnp.dot(hidden_act, w_down, preferred_element_type=jnp....  413 us
    all_gather x2, waiting for transfers between devices, body(): lax.all_gather(own_rows, ('section', 'vocab'), axis=0, tiled=True)  123 us
    dot_general x2, matrix products, body(): logits = jnp.dot(scaled, head_weight, preferred_element_type=jnp.float32)  56.4 us
    psum x1, waiting for transfers between devices, body(): lax.psum(jnp.dot(hidden_act, w_down, preferred_element_type=jnp.float32),...  52.2 us
    psum x1, blocking collectives, body(): seq_logprob = lax.psum(jnp.stack(partials), ('section', 'vocab'))  40.4 us
    dot_general x2, matrix products, body(): jnp.dot(hidden_act, w_down, preferred_element_type=jnp.float32)  39 us
  transfers between devices with their start and end apart: 12, of which 10 were waited for; matrix products, arithmetic and copies ran while one was open for 24% of the time, Pallas kernels for 0%

profile of v1, /device:TPU:0, one launch (start us, length us, event | category | flops | bytes accessed | tf_op | source)
XLA Modules:
  0.0 1460.1 jit_solution(1780830453203538435)
XLA Ops:
  9.7 64.3 %all-gather.5.cloned.1.call-done = bf16[1,256,7168]{2,1,0:T(8,128)(2,1)} async-done(((bf16[1,8,7168]{2,1,0:T(8,128)(2,1)}), bf16[1,256,7168]{2,1,0:T(8,128)(2,1)}) %all-gather.5.cloned.1.call-update) | async-done | bytes 3670032 | tf_op jit(solution)/shard_map/all_gather | solution.py:50
  74.0 2.8 fusion.6
  76.9 59.1 %all-gather.7.cloned.1.call-done = bf16[1,256,7168]{2,1,0:T(8,128)(2,1)} async-done(((bf16[1,8,7168]{2,1,0:T(8,128)(2,1)}), bf16[1,256,7168]{2,1,0:T(8,128)(2,1)}) %all-gather.7.cloned.1.call-update) | async-done | bytes 3670032 | tf_op jit(solution)/shard_map/all_gather | solution.py:50
  135.9 3.0 fusion.10
  139.0 7.0 fusion.28
  148.5 19.6 %fusion.34 = f32[256,7168]{1,0:T(8,128)} fusion(bf16[576,7168]{1,0:T(8,128)(2,1)} %param.13, bf16[7168,576]{0,1:T(8,128)(2,1)} %param.12, bf16[1,256,7168]{2,1,0:T(8,128)(2,1)} %all-gather.5.cloned.1.call-done, f32[7168]{0:T(1024)S(1)} %copy-done.3, f32[256]{0:T(256)S(1)} %add_rsqrt_fusion.3, f32[256,576]{0,1:T(8,128)S(1)} %fusion.28), kind=kOutput, calls=%fused_computation.41 | convolution fusion | flops 4236083200 | bytes 28144640 | tf_op jit(solution)/shard_map/dot_general | solution.py:56
  168.1 19.4 %fusion.31 = f32[256,7168]{1,0:T(8,128)} fusion(bf16[576,7168]{1,0:T(8,128)(2,1)} %param.13, bf16[7168,576]{0,1:T(8,128)(2,1)} %param.12, bf16[1,256,7168]{2,1,0:T(8,128)(2,1)} %all-gather.7.cloned.1.call-done, f32[256]{0:T(256)S(1)} %add_rsqrt_fusion.1, f32[7168]{0:T(1024)S(1)} %copy-done.3, f32[256,576]{0,1:T(8,128)S(1)} %fusion.25), kind=kOutput, calls=%fused_computation.40 | convolution fusion | flops 4236083200 | bytes 28144640 | tf_op jit(solution)/shard_map/dot_general | solution.py:56
  188.0 52.2 %all-reduce.7.cloned.1.call-done = (f32[256,7168]{1,0:T(8,128)}, f32[256,7168]{1,0:T(8,128)}) async-done(((f32[256,7168]{1,0:T(8,128)}, f32[256,7168]{1,0:T(8,128)}), (f32[256,7168]{1,0:T(8,128)}, f32[256,7168]{1,0:T(8,128)})) %all-reduce.7.cloned.1.call-update) | async-done | bytes 14680080 | tf_op jit(solution)/shard_map/psum | solution.py:56
  240.9 413.4 %all-reduce.5.cloned.1.call-done = (f32[256,7168]{1,0:T(8,128)}, f32[256,7168]{1,0:T(8,128)}) async-done(((f32[256,7168]{1,0:T(8,128)}, f32[256,7168]{1,0:T(8,128)}), (f32[256,7168]{1,0:T(8,128)}, f32[256,7168]{1,0:T(8,128)})) %all-reduce.5.cloned.1.call-update) | async-done | bytes 14680080 | tf_op jit(solution)/shard_map/psum | solution.py:55
  654.3 8.4 fusion
  662.7 28.2 %fusion.46 = (f32[256]{0:T(256)S(1)}, f32[256,4040]{0,1:T(8,128)}) fusion(bf16[7168,4040]{0,1:T(8,128)(2,1)} %param.15, f32[7168]{0:T(1024)S(1)} %copy-done.4, f32[256]{0:T(256)S(1)} %add_rsqrt_fusion.2, f32[256,7168]{1,0:T(8,128)} %get-tuple-element.25, bf16[1,256,7168]{2,1,0:T(8,128)(2,1)} %all-gather.5.cloned.1.call-done), kind=kOutput, calls=%fused_computation.75 | convolution fusion | flops 14840743936 | bytes 73095168 | tf_op jit(solution)/shard_map/dot_general | solution.py:61
  693.1 296.8 %sort.56 = (f32[256,4040]{0,1:T(8,128)}, s32[256,4040]{0,1:T(8,128)}) sort(f32[256,4040]{0,1:T(8,128)} %get-tuple-element.41, s32[256,4040]{0,1:T(8,128)} %iota.24.clone), dimensions={1}, to_apply=%region_20.21 | sort | flops 20684800 | bytes 16547840 | tf_op jit(solution)/shard_map/sort | solution.py:18
  990.0 5.6 copy.39
  996.2 3.2 all-to-all-start.1
  999.5 28.2 %fusion.47 = (f32[256]{0:T(256)S(1)}, f32[256,4040]{0,1:T(8,128)}) fusion(bf16[7168,4040]{0,1:T(8,128)(2,1)} %param.15, f32[256]{0:T(256)S(1)} %add_rsqrt_fusion, f32[7168]{0:T(1024)S(1)} %copy-done.4, f32[256,7168]{1,0:T(8,128)} %get-tuple-element.24, bf16[1,256,7168]{2,1,0:T(8,128)(2,1)} %all-gather.7.cloned.1.call-done), kind=kOutput, calls=%fused_computation.76 | convolution fusion | flops 14840743936 | bytes 73095168 | tf_op jit(solution)/shard_map/dot_general | solution.py:61
  1027.7 5.1 exponential_reduce_fusion.1
  1033.7 296.8 %sort.58 = (f32[256,4040]{0,1:T(8,128)}, s32[256,4040]{0,1:T(8,128)}) sort(f32[256,4040]{0,1:T(8,128)} %get-tuple-element.43, s32[256,4040]{0,1:T(8,128)} %iota.24.clone), dimensions={1}, to_apply=%region_23.24 | sort | flops 20684800 | bytes 16547840 | tf_op jit(solution)/shard_map/sort | solution.py:18
  1331.2 5.5 copy.43
  1336.8 5.8 all-to-all-start.2
  1349.8 4.0 all-to-all-start
  1353.8 7.1 all-to-all-done
  1360.9 2.5 all-to-all-start.4
  1363.5 7.1 all-to-all-done.4
  1370.6 2.5 all-to-all-start.5
  1373.2 7.1 all-to-all-done.5
  1380.3 2.5 all-to-all-start.3
  1382.8 7.1 all-to-all-done.3
  1389.9 2.5 all-to-all-start.6
  1393.8 40.4 %psum.39 = f32[2,8]{1,0:T(2,128)} all-reduce(f32[2,8]{1,0:T(2,128)S(1)} %pad_maximum_fusion.3), channel_id=1, replica_groups=mesh['section'=2,'vocab'=16] {'section','vocab'}, use_global_device_ids=true, to_apply=%region_28.29 | all-reduce | flops 16 | bytes 128 | tf_op jit(solution)/shard_map/psum | solution.py:95
  1434.2 5.0 all-to-all-start.7
  1440.7 4.9 sort.57
  1447.4 4.9 sort.59
  (76 shorter events, 23.5 us)
Async XLA Ops:
  7.2 131.8 %copy-start.3 = (f32[7168]{0:T(1024)S(1)}, f32[7168]{0:T(1024)}, u32[]{:S(2)}) copy-start(f32[7168]{0:T(1024)} %param.10) | copy-start | bytes 86020
  7.2 66.8 %all-gather.5.cloned.1.call-start = ((), (), s32[]{:S(2)}) async-start(), calls=%async_computation.8 | async-start | bytes 3784704 | tf_op jit(solution)/shard_map/all_gather | solution.py:50
  8.9 127.0 %all-gather.7.cloned.1.call-start = ((), (), s32[]{:S(2)}) async-start(), calls=%async_computation.9 | async-start | bytes 3784704 | tf_op jit(solution)/shard_map/all_gather | solution.py:50
  9.6 230.6 %all-reduce.7.cloned.1.call-start = ((), (), s32[]{:S(2)}) async-start(), calls=%async_computation.11 | async-start | bytes 29360128 | tf_op jit(solution)/shard_map/psum | solution.py:56
  135.9 10.1 slice-start
  138.9 7.1 copy-start
  139.0 7.1 slice-start.1
  187.5 466.8 %all-reduce.5.cloned.1.call-start = ((), (), s32[]{:S(2)}) async-start(), calls=%async_computation.10 | async-start | bytes 29360128 | tf_op jit(solution)/shard_map/psum | solution.py:55
  240.2 0.7 copy-start.2
  240.2 0.7 copy-start.1
  654.3 8.4 copy-start.4
  996.2 340.5 %all-to-all-start.1 = ((f32[32,1,8]{2,1,0:T(1,128)}), f32[32,1,8]{2,1,0:T(1,128)S(1)}, u32[]{:S(2)}, u32[]{:S(2)}) async-start(f32[32,1,8]{2,1,0:T(1,128)} %bitcast.5), calls=%async_computation.1 | async-start | bytes 32768 | tf_op jit(solution)/shard_map/all_to_all | solution.py:74
  1336.8 13.0 all-to-all-start.2
  1349.8 11.2 all-to-all-start
  1360.9 9.7 all-to-all-start.4
  1370.6 9.6 all-to-all-start.5
  1380.3 9.6 all-to-all-start.3
  1389.9 44.3 %all-to-all-start.6 = ((f32[32,1,160]{2,1,0:T(1,128)}), f32[32,1,160]{2,1,0:T(1,128)S(1)}, u32[]{:S(2)}, u32[]{:S(2)}) async-start(f32[32,1,160]{2,1,0:T(1,128)} %reshape.189), calls=%async_computation.6 | async-start | bytes 65536 | tf_op jit(solution)/shard_map/all_to_all | solution.py:83
  1434.2 12.2 all-to-all-start.7
Sparse Core Ops, SparseCore 0:
  10.8 63.1 all-gather.4
  76.9 59.0 all-gather.6
  187.6 52.5 all-reduce.6
  246.5 407.7 all-reduce.4
